TPU v7x, 32 devices: a whole 2x2x4 slice. The times are simulated.
32 devices in a mesh: fsdp: 4 (over z), ctx: 2 (over y), tp: 4 (over x, core).
Axes of the slice: x: 2, y: 2, z: 4, core: 2. Of those that a mesh axis runs over, the one named last changes fastest.
Arguments:
- layer_input: bfloat16 [8192, 768], P(('fsdp', 'ctx')), may hold values from -6 to 6
- segments: int32 [8192], P('fsdp'), may hold values from 0 to 7, as said below
- positions: int32 [8192], P(('fsdp', 'ctx')), may hold values from 0 to 1535, as said below
- ln1_gain: float32 [768], replicated, may hold values from 0.1 to 1.9
- ln1_bias: float32 [768], replicated, may hold values from -3 to 3
- ln2_gain: float32 [768], replicated, may hold values from 0.1 to 1.9
- ln2_bias: float32 [768], replicated, may hold values from -3 to 3
- w_qkv: bfloat16 [768, 3, 768], P('fsdp', None, 'tp'), as said below
- b_qkv: float32 [3, 768], P(None, 'tp'), may hold values from -3 to 3
- w_out: bfloat16 [768, 768], P('tp', 'fsdp'), may hold values from -1.75 to 1.75
- b_out: float32 [768], replicated, may hold values from -3 to 3
- w_fc1: bfloat16 [768, 3072], P('fsdp', 'tp'), may hold values from -0.21875 to 0.21875
- b_fc1: float32 [3072], P('tp'), may hold values from -3 to 3
- w_fc2: bfloat16 [3072, 768], P('tp', 'fsdp'), may hold values from -0.109375 to 0.109375
- b_fc2: float32 [768], replicated, may hold values from -3 to 3
- out_grad: float32 [8192, 768], P(('fsdp', 'ctx')), may hold values from -6 to 6
Outputs:
- block_out: float32 [8192, 768], P(('fsdp', 'ctx'))
- input_grad: float32 [8192, 768], P(('fsdp', 'ctx'))
- g_ln1_gain: float32 [768], replicated
- g_ln1_bias: float32 [768], replicated
- g_ln2_gain: float32 [768], replicated
- g_ln2_bias: float32 [768], replicated
- g_w_qkv: float32 [768, 3, 768], P('fsdp', None, 'tp')
- g_b_qkv: float32 [3, 768], P(None, 'tp')
- g_w_out: float32 [768, 768], P('tp', 'fsdp')
- g_b_out: float32 [768], replicated
- g_w_fc1: float32 [768, 3072], P('fsdp', 'tp')
- g_b_fc1: float32 [3072], P('tp')
- g_w_fc2: float32 [3072, 768], P('tp', 'fsdp')
- g_b_fc2: float32 [768], replicated
Inputs may be any that keep to these rules, and one draw needn't show every extreme that they name: `segments`: within each sequence of 2048 tokens the numbers never fall, start at 0, and every value up to 7 appears; document 0 covers exactly the first 1536 tokens of each sequence. `positions`: the offset of a token from the first token of its document. `w_qkv`: entries of order 768 ** -0.5, up to a factor of a few.
All inputs are finite; a program needn't handle non-finite values.
Results may differ from a plain program's by a relative error of at most 0.012.
Values may be sent and summed in bfloat16 or wider, within the bound.
A program may use at most 128 MiB of HBM per device.

v0:
```python
import jax
import jax.numpy as jnp
from jax import lax
from jax.experimental import pallas as pl
from jax.experimental.pallas import tpu as pltpu
from jax.sharding import PartitionSpec as P

HD = 64
ROT = 16
HALF = ROT // 2
NEG_FILL = -1e30
NORM_EPS = 1e-05
INV_ROOT_TWO = 0.7071067811865476
INV_ROOT_TWO_PI = 0.3989422804014327
F32 = jnp.float32
BF16 = jnp.bfloat16
VMEM_BYTES = 67043328


def mm(a, b):
    return jnp.dot(a, b, preferred_element_type=F32)


def mm_nt(a, b):
    return lax.dot_general(a, b, (((1,), (1,)), ((), ())), preferred_element_type=F32)


def tile_rows(i, size):
    return pl.ds(pl.multiple_of(i * size, size), size)


class Dims:
    def __init__(self, mesh, tokens, width, span, hidden):
        self.nz, self.nc, self.nt = mesh.shape["fsdp"], mesh.shape["ctx"], mesh.shape["tp"]
        self.tok, self.width, self.span, self.hidden = tokens, width, span, hidden
        self.heads = span // HD
        self.blk = min(512, tokens)
        self.nb = tokens // self.blk
        self.nkb = self.nc * self.nb
        self.tail = (3 * self.nkb) // 4
        self.rows = width // self.nz
        self.half = self.rows // 2
        self.tile = min(256, tokens)
        self.nx = self.nt // 2
        self.keep = self.nc <= 2
        assert 4 * span == hidden and self.nt % 2 == 0 and self.nc % 2 == 0
        self.wide = max(width, hidden, 3 * span)
        nz, nc, nx = self.nz, self.nc, self.nx
        self.n_copies = (
            3 * 2 * (nz - 1)
            + 2 * (nc - 1)
            + 2 * (nx + 1)
            + 3 * (1 + (nz - 1) + (nc - 1))
            + (nz * nc - 1)
            + (self.nt - 1)
        )


class Net:
    def __init__(self, send, recv):
        self.send, self.recv, self.used, self.started = send, recv, 0, []

    def copy(self, src, dst, device):
        i = self.used
        self.used += 1
        return pltpu.make_async_remote_copy(
            src_ref=src,
            dst_ref=dst,
            send_sem=self.send.at[i],
            recv_sem=self.recv.at[i],
            device_id=device,
            device_id_type=pl.DeviceIdType.MESH,
        )


def layer_kernel(d, *refs):
    (x, og, pos, cosr, sinr, vec, bq, bf1, wa, wb, wc) = refs[:11]
    (out, ig, ga, gb_out, gc_out, sm_out) = refs[11:17]
    (
        WA, WB, WC, WT, h1, h2, tA, gb, gbT, mean_s, inv_s, act, dpre,
        qz, kv, kvn, doz, ctxT, lse, dlt, dq, dkv,
        ra, chU, chE, finU, finE,
        ggB, ggC, r1A, r1B, r1C, r2A, r2B, r2C, f3A, f3B, f3C,
        sm, smr, smt, send, recv,
    ) = refs[17:]
    ub, ggA = h2, ggB
    T, D, hs, F = d.tok, d.width, d.span, d.hidden
    nz, nc, nt, nx = d.nz, d.nc, d.nt, d.nx
    heads, B, nb, R, HR, TB = d.heads, d.blk, d.nb, d.rows, d.half, d.tile
    z, c, t = lax.axis_index("fsdp"), lax.axis_index("ctx"), lax.axis_index("tp")
    part = lax.rem(c, 2)
    other = 1 - part
    pair = c + 1 - 2 * part
    core = lax.rem(t, 2)
    xg = t // 2
    mate = t + 1 - 2 * core
    net = Net(send, recv)
    scale = HD ** (-0.5)

    def turn(value, step, size):
        return lax.rem(value + step, size)

    barrier = pltpu.get_barrier_semaphore()
    talks = []
    for rz in range(nz):
        for rc in range(nc):
            if rz or rc:
                talks.append((turn(z, rz, nz), turn(c, rc, nc), t))
    for rt in range(1, nt):
        talks.append((z, c, turn(t, rt, nt)))
    for device in talks:
        pl.semaphore_signal(barrier, inc=1, device_id=device, device_id_type=pl.DeviceIdType.MESH)
    pl.semaphore_wait(barrier, len(talks))

    half_here = pl.ds(pl.multiple_of(part * HR, HR), HR)

    def rows_of(src):
        return pl.ds(pl.multiple_of(src * R + part * HR, HR), HR)

    gathers = []
    for shard, full in ((wa, WA), (wb, WB), (wc, WC)):
        first = [
            net.copy(shard.at[half_here], full.at[rows_of(z)], (turn(z, r, nz), c, t))
            for r in range(1, nz)
        ]
        second = []
        for r in range(1, nz):
            src = turn(z, nz - r, nz)
            second.append(net.copy(full.at[rows_of(src)], full.at[rows_of(src)], (z, pair, t)))
        gathers.append((first, second))
        for one in first:
            one.start()

    def relay(i):
        for one, two in zip(*gathers[i]):
            one.wait_recv()
            two.start()

    def gathered(i):
        for two in gathers[i][1]:
            two.wait_recv()

    sm[...] = jnp.zeros_like(sm)
    g1, b1, g2, b2 = vec[0:1, :], vec[1:2, :], vec[2:3, :], vec[3:4, :]

    def norm_tile(i, carry):
        rows = tile_rows(i, TB)
        xf = x[rows, :].astype(F32)
        mean = jnp.mean(xf, -1, keepdims=True)
        cen = xf - mean
        inv = lax.rsqrt(jnp.mean(cen * cen, -1, keepdims=True) + NORM_EPS)
        normed = cen * inv
        mean_s[rows, :] = mean
        inv_s[rows, :] = inv
        h1[rows, :] = (normed * g1 + b1).astype(BF16)
        h2[rows, :] = (normed * g2 + b2).astype(BF16)
        grad = og[rows, :]
        gb[rows, :] = grad.astype(BF16)
        sm[4:5, :D] += jnp.sum(grad, 0, keepdims=True)
        return carry

    lax.fori_loop(0, T // TB, norm_tile, 0)
    own_rows = pl.ds(pl.multiple_of(z * R, R), R)
    WA[own_rows, :] = wa[...]
    WB[own_rows, :] = wb[...]
    WC[own_rows, :] = wc[...]
    for i in range(nb):
        gbT[i] = jnp.transpose(gb[i * B : (i + 1) * B, :])
        tA[:, i * B : (i + 1) * B] = jnp.transpose(h2[i * B : (i + 1) * B, :])

    relay(0)
    gathered(0)
    WT[...] = jnp.transpose(WA[...])

    for i in range(nb):
        proj = mm_nt(WT[: 3 * hs, :], h1[i * B : (i + 1) * B, :]) + bq[...]
        cb, sb = cosr[i], sinr[i]

        def rotated(tensor):
            lo, hi = tensor[:HALF], tensor[HALF:ROT]
            return jnp.concatenate([lo * cb - hi * sb, hi * cb + lo * sb, tensor[ROT:]], 0)

        own = c * nb + i
        for h in range(heads):
            q = rotated(proj[h * HD : (h + 1) * HD]).astype(BF16) * jnp.asarray(scale, BF16)
            qz[i, h] = jnp.concatenate([q, jnp.zeros_like(q)], 0)
            key = rotated(proj[hs + h * HD : hs + (h + 1) * HD]).astype(BF16)
            value = proj[2 * hs + h * HD : 2 * hs + (h + 1) * HD].astype(BF16)
            both = jnp.concatenate([key, value], 0)
            kv[own, h] = both
            if d.keep:
                kvn[own, h] = jnp.transpose(both)

    own_blocks = pl.ds(c * nb, nb)
    kv_out = [
        net.copy(kv.at[own_blocks], kv.at[own_blocks], (z, turn(c, r, nc), t))
        for r in range(1, nc)
    ]
    for r, one in enumerate(kv_out, 1):

        @pl.when(c + r < nc)
        def _(one=one):
            one.start()

    relay(1)

    for i in range(nb):
        dct = mm(WT[3 * hs :, :], gbT[i]).astype(BF16)
        for h in range(heads):
            piece = dct[h * HD : (h + 1) * HD]
            doz[i, h] = jnp.concatenate([jnp.zeros_like(piece), piece], 0)

    relay(2)
    gathered(1)
    gathered(2)

    def normed_of(rows):
        return (x[rows, :].astype(F32) - mean_s[rows, :]) * inv_s[rows, :]

    def mlp_tile(i, carry):
        rows = tile_rows(i, TB)
        pre = mm(h2[rows, :], WB[...]) + bf1[...]
        cdf = 0.5 * (1.0 + lax.erf(pre * INV_ROOT_TWO))
        density = jnp.exp(-0.5 * pre * pre) * INV_ROOT_TWO_PI
        actb = (pre * cdf).astype(BF16)
        act[rows, :] = actb
        dp = mm(gb[rows, :], WC[...]) * (cdf + pre * density)
        sm[5:6, :F] += jnp.sum(dp, 0, keepdims=True)
        dpb = dp.astype(BF16)
        dpre[rows, :] = dpb
        out[rows, :] = mm_nt(actb, WC[...])
        dh2 = mm_nt(dpb, WB[...])
        sm[2:3, :D] += jnp.sum(dh2 * normed_of(rows), 0, keepdims=True)
        sm[3:4, :D] += jnp.sum(dh2, 0, keepdims=True)
        ig[rows, :] = dh2 * g2
        return carry

    lax.fori_loop(0, T // TB, mlp_tile, 0)

    def store_grad(gg, value, z0):
        for k in range(value.shape[0] // HR):
            gg[k % 2, z0 + k // 2] = value[k * HR : (k + 1) * HR].astype(BF16)

    class Reduce:
        def __init__(self, gg, r1, r2, f3, final):
            self.gg, self.r1, self.r2, self.f3, self.final = gg, r1, r2, f3, final
            self.a = net.copy(gg.at[other], r1, (z, pair, t))
            self.b = [
                net.copy(gg.at[part, turn(z, r, nz)], r2.at[r - 1], (turn(z, r, nz), c, t))
                for r in range(1, nz)
            ]
            self.c = [net.copy(f3.at[c], f3.at[c], (z, turn(c, r, nc), t)) for r in range(1, nc)]

        def one(self):
            self.a.start()

        def two(self):
            self.a.wait_recv()
            for r in range(1, nz):
                zz = turn(z, r, nz)
                self.gg[part, zz] = (self.gg[part, zz].astype(F32) + self.r1[zz].astype(F32)).astype(BF16)
                self.b[r - 1].start()

        def three(self):
            total = self.gg[part, z].astype(F32) + self.r1[z].astype(F32)
            for r in range(1, nz):
                self.b[r - 1].wait_recv()
                total += self.r2[r - 1].astype(F32)
            self.f3[c] = total.astype(BF16)
            for one in self.c:
                one.start()

        def four(self):
            for one in self.c:
                one.wait_recv()
            for p in range(2):
                total = self.f3[p].astype(F32)
                for j in range(1, nc // 2):
                    total += self.f3[2 * j + p].astype(F32)
                self.final[p * HR : (p + 1) * HR, :] = total

        def drain(self):
            for one in [self.a, *self.b, *self.c]:
                one.wait_send()

    redB = Reduce(ggB, r1B, r2B, f3B, gb_out)
    redC = Reduce(ggC, r1C, r2C, f3C, gc_out)
    redA = Reduce(ggA, r1A, r2A, f3A, ga)

    for z0 in range(0, nz, 2):
        store_grad(ggB, mm(tA[z0 * R : (z0 + 2) * R, :], dpre[...]), z0)
    redB.one()
    for z0 in range(0, nz, 2):
        value = None
        for i in range(nb):
            term = mm(gbT[i, z0 * R : (z0 + 2) * R, :], act[i * B : (i + 1) * B, :])
            value = term if value is None else value + term
        store_grad(ggC, value, z0)
    redC.one()

    for r, one in enumerate(kv_out, 1):

        @pl.when(c >= r)
        def _(r=r, one=one):
            one.wait_recv()

            def flip(j, carry):
                at = (c - r) * nb + j
                for h in range(heads):
                    kvn[at, h] = jnp.transpose(kv[at, h])
                return carry

            if d.keep:
                lax.fori_loop(0, nb, flip, 0)

    def natural(at, h):
        return kvn[at, h] if d.keep else jnp.transpose(kv[at, h])

    def allowed_of(i, at):
        query_at = (c * nb + i) * B + lax.broadcasted_iota(jnp.int32, (1, B), 1)
        key_at = at * B + lax.broadcasted_iota(jnp.int32, (B, 1), 0)
        return (key_at <= query_at) & (key_at >= query_at - pos[i])

    for i in range(nb):
        here = c * nb + i
        first_key = jnp.where(here >= d.tail, d.tail, 0)
        for h in range(heads):
            qh = qz[i, h]

            def key_step(at, carry, i=i, h=h, qh=qh):
                top, total, weighted = carry
                s = jnp.where(allowed_of(i, at), mm(natural(at, h), qh), NEG_FILL)
                new_top = jnp.maximum(top, jnp.max(s, 0, keepdims=True))
                w = jnp.exp(s - new_top)
                factor = jnp.exp(top - new_top)
                total = total * factor + jnp.sum(w, 0, keepdims=True)
                weighted = weighted * factor + mm(kv[at, h, HD:], w.astype(BF16))
                return new_top, total, weighted

            top, total, weighted = lax.fori_loop(
                first_key,
                here + 1,
                key_step,
                (
                    jnp.full((1, B), NEG_FILL, F32),
                    jnp.zeros((1, B), F32),
                    jnp.zeros((HD, B), F32),
                ),
            )
            lse[i, h : h + 1, :] = top + jnp.log(total)
            ctx_h = (weighted / total).astype(BF16)
            ctxT[i, h * HD : (h + 1) * HD, :] = ctx_h
            dlt[i, h : h + 1, :] = jnp.sum(
                doz[i, h, HD:].astype(F32) * ctx_h.astype(F32), 0, keepdims=True
            )

    class Join:
        def __init__(self, ra, ch, fin):
            self.ra, self.ch, self.fin = ra, ch, fin
            self.near = net.copy(
                ub.at[pl.ds(pl.multiple_of((1 - core) * (T // 2), T // 2), T // 2)], ra, (z, c, mate)
            )
            self.far = [
                net.copy(ch.at[xg], ch.at[xg], (z, c, turn(xg, r, nx) * 2 + core))
                for r in range(1, nx)
            ]
            self.back = net.copy(fin.at[core], fin.at[core], (z, c, mate))

        def one(self):
            self.near.start()

        def two(self):
            self.near.wait_recv()
            for k in range(T // 2 // TB):
                mine = pl.ds(pl.multiple_of(core * (T // 2) + k * TB, TB), TB)
                tile = slice(k * TB, (k + 1) * TB)
                self.ch[xg, tile, :] = (
                    ub[mine, :].astype(F32) + self.ra[tile, :].astype(F32)
                ).astype(BF16)
            for one in self.far:
                one.start()

        def three(self):
            for one in self.far:
                one.wait_recv()
            for k in range(T // 2 // TB):
                tile = slice(k * TB, (k + 1) * TB)
                total = self.ch[0, tile, :].astype(F32)
                for j in range(1, nx):
                    total += self.ch[j, tile, :].astype(F32)
                self.fin[core, tile, :] = total.astype(BF16)
            self.back.start()

        def four(self):
            self.back.wait_recv()

        def drain(self):
            for one in [*self.far, self.back]:
                one.wait_send()

    join_u = Join(ra, chU, finU)
    join_e = Join(ra, chE, finE)

    for i in range(nb):
        ctx_n = jnp.transpose(ctxT[i])
        for k in range(B // TB):
            rows = slice(i * B + k * TB, i * B + (k + 1) * TB)
            ub[rows, :] = (
                out[rows, :] + mm(ctx_n[k * TB : (k + 1) * TB], WT[3 * hs :, :])
            ).astype(BF16)
    join_u.one()
    redB.two()
    redC.two()

    dq[...] = jnp.zeros_like(dq)

    def key_back(at, h, put):
        k_t = kv[at, h, :HD]
        k_n = natural(at, h)

        def query_step(i, carry):
            dk, dv = carry
            s = mm(k_n, qz[i, h])
            ok = allowed_of(i, at)
            prob = jnp.where(ok, jnp.exp(s - lse[i, h : h + 1, :]), 0.0)
            dp = mm(k_n, doz[i, h])
            ds = (prob * (dp - dlt[i, h : h + 1, :])).astype(BF16)
            dv = dv + mm_nt(doz[i, h, HD:], prob.astype(BF16))
            dk = dk + mm_nt(qz[i, h, :HD], ds)
            dq[i, h] += mm(k_t, ds)
            return dk, dv

        begin = jnp.maximum(at - c * nb, 0)
        end = jnp.where(at < d.tail, jnp.minimum(nb, d.tail - c * nb), nb)
        zero = jnp.zeros((HD, B), F32)
        put(lax.fori_loop(begin, end, query_step, (zero, zero)))

    dkv_out = []
    for r in range(1, nc):
        owner = turn(c, nc - r, nc)
        dkv_out.append(net.copy(kv.at[pl.ds(owner * nb, nb)], kv.at[own_blocks], (z, owner, t)))
    for r in reversed(range(1, nc)):

        @pl.when(c >= r)
        def _(r=r):
            def block(j, carry):
                for h in range(heads):

                    def put(pieces, h=h):
                        kv[(c - r) * nb + j, h, :HD] = pieces[0].astype(BF16)
                        kv[(c - r) * nb + j, h, HD:] = pieces[1].astype(BF16)

                    key_back((c - r) * nb + j, h, put)
                return carry

            lax.fori_loop(0, nb, block, 0)
            dkv_out[r - 1].start()

    join_u.two()

    def own_block(j, carry):
        for h in range(heads):

            def put(pieces, h=h):
                dkv[j, h, :HD] = pieces[0]
                dkv[j, h, HD:] = pieces[1]

            key_back(c * nb + j, h, put)
        return carry

    lax.fori_loop(0, nb, own_block, 0)
    redB.three()
    redC.three()
    join_u.three()

    for r in range(1, nc):

        @pl.when(c + r < nc)
        def _(r=r):
            dkv_out[r - 1].wait_recv()
            for j in range(nb):
                for h in range(heads):
                    dkv[j, h] += kv[(c + r) * nb + j, h].astype(F32)

    grad_t = None
    bias_t = jnp.zeros((3 * hs, 1), F32)
    for i in range(nb):
        cb, sb = cosr[i], sinr[i]

        def unrotated(g):
            lo, hi = g[:HALF], g[HALF:ROT]
            return jnp.concatenate([lo * cb + hi * sb, hi * cb - lo * sb, g[ROT:]], 0)

        pieces = [unrotated(dq[i, h] * scale) for h in range(heads)]
        pieces += [unrotated(dkv[i, h, :HD]) for h in range(heads)]
        pieces += [dkv[i, h, HD:] for h in range(heads)]
        d_proj = jnp.concatenate(pieces, 0)
        bias_t += jnp.sum(d_proj, -1, keepdims=True)
        d_proj_b = d_proj.astype(BF16)
        tA[: 3 * hs, i * B : (i + 1) * B] = d_proj_b
        act[i * B : (i + 1) * B, : 3 * hs] = jnp.transpose(d_proj_b)
    sm[6:7, : 3 * hs] = jnp.transpose(jnp.broadcast_to(bias_t, (3 * hs, 128)))[0:1, :]

    grad_q = mm(tA[: 3 * hs, :], h1[...])
    grad_o = None
    for i in range(nb):
        term = mm(ctxT[i], gb[i * B : (i + 1) * B, :])
        grad_o = term if grad_o is None else grad_o + term
    grad_a = jnp.transpose(jnp.concatenate([grad_q.astype(BF16), grad_o.astype(BF16)], 0))
    for one in [redB.a, *redB.b]:
        one.wait_send()
    store_grad(ggA, grad_a, 0)
    redA.one()
    join_u.near.wait_send()

    def e_tile(i, carry):
        rows = tile_rows(i, TB)
        dh1 = mm(act[rows, : 3 * hs], WT[: 3 * hs, :])
        sm[0:1, :D] += jnp.sum(dh1 * normed_of(rows), 0, keepdims=True)
        sm[1:2, :D] += jnp.sum(dh1, 0, keepdims=True)
        ub[rows, :] = (ig[rows, :] + dh1 * g1).astype(BF16)
        return carry

    lax.fori_loop(0, T // TB, e_tile, 0)
    join_u.four()
    join_e.one()

    rank = z * nc + c
    smr[rank] = sm[...]
    small_a = []
    for rz in range(nz):
        for rc in range(nc):
            if rz or rc:
                small_a.append(
                    net.copy(smr.at[rank], smr.at[rank], (turn(z, rz, nz), turn(c, rc, nc), t))
                )
    for one in small_a:
        one.start()
    join_e.two()
    redA.two()

    def out_tile(i, carry):
        rows = tile_rows(i, TB)
        per = T // 2 // TB
        total = finU[i // per, tile_rows(lax.rem(i, per), TB), :].astype(F32)
        out[rows, :] = x[rows, :].astype(F32) + total + vec[4:5, :]
        return carry

    lax.fori_loop(0, T // TB, out_tile, 0)
    redB.four()
    redC.four()

    for one in small_a:
        one.wait_recv()
    tot = smr[0]
    for j in range(1, nz * nc):
        tot += smr[j]
    smt[t] = tot
    small_b = [net.copy(smt.at[t], smt.at[t], (z, c, turn(t, r, nt))) for r in range(1, nt)]
    for one in small_b:
        one.start()
    redA.three()
    join_e.three()
    for one in small_b:
        one.wait_recv()
    tops = smt[0, 0:4, :]
    for j in range(1, nt):
        tops += smt[j, 0:4, :]
    sm_out[...] = jnp.concatenate([tops, tot[4:8, :]], 0)
    join_e.four()

    def in_tile(i, carry):
        rows = tile_rows(i, TB)
        per = T // 2 // TB
        e = finE[i // per, tile_rows(lax.rem(i, per), TB), :].astype(F32)
        normed = normed_of(rows)
        ig[rows, :] = og[rows, :] + inv_s[rows, :] * (
            e
            - jnp.mean(e, -1, keepdims=True)
            - normed * jnp.mean(e * normed, -1, keepdims=True)
        )
        return carry

    lax.fori_loop(0, T // TB, in_tile, 0)
    redA.four()

    for first, second in gathers:
        for one in [*first, *second]:
            one.wait_send()
    for r, one in enumerate(kv_out, 1):

        @pl.when(c + r < nc)
        def _(one=one):
            one.wait_send()

    for r, one in enumerate(dkv_out, 1):

        @pl.when(c >= r)
        def _(one=one):
            one.wait_send()

    for one in redB.c:
        one.wait_send()
    redA.drain()
    redC.drain()
    join_u.drain()
    join_e.near.wait_send()
    join_e.drain()
    for one in [*small_a, *small_b]:
        one.wait_send()
    assert net.used == d.n_copies


def body(
    mesh,
    layer_input,
    segments,
    positions,
    ln1_gain,
    ln1_bias,
    ln2_gain,
    ln2_bias,
    w_qkv,
    b_qkv,
    w_out,
    b_out,
    w_fc1,
    b_fc1,
    w_fc2,
    b_fc2,
    out_grad,
):
    d = Dims(mesh, layer_input.shape[0], layer_input.shape[1], b_qkv.shape[1], b_fc1.shape[0])
    T, D, hs, F, B, nb = d.tok, d.width, d.span, d.hidden, d.blk, d.nb
    R, HR, nz, nc = d.rows, d.half, d.nz, d.nc
    freqs = 10000.0 ** (-(jnp.arange(HALF, dtype=F32) * 2.0) / ROT)
    angles = positions.astype(F32).reshape(nb, 1, B) * freqs[None, :, None]
    vec = jnp.stack([ln1_gain, ln1_bias, ln2_gain, ln2_bias, b_out + b_fc2] + [ln1_gain] * 3)
    wide_a = 4 * hs
    args = (
        layer_input,
        out_grad,
        positions.reshape(nb, 1, B),
        jnp.cos(angles),
        jnp.sin(angles),
        vec,
        b_qkv.reshape(3 * hs, 1),
        b_fc1.reshape(1, F),
        jnp.concatenate([w_qkv.reshape(R, 3 * hs), w_out.T], 1),
        w_fc1,
        w_fc2.T,
    )
    vm = pltpu.VMEM
    h, W = d.heads, d.wide
    scratch = [
        vm((D, wide_a), BF16), vm((D, F), BF16), vm((D, F), BF16), vm((wide_a, D), BF16),
        vm((T, D), BF16), vm((T, D), BF16), vm((D, T), BF16), vm((T, D), BF16), vm((nb, D, B), BF16),
        vm((T, 1), F32), vm((T, 1), F32), vm((T, F), BF16), vm((T, F), BF16),
        vm((nb, h, 2 * HD, B), BF16), vm((d.nkb, h, 2 * HD, B), BF16), vm((d.nkb if d.keep else 1, h, B, 2 * HD), BF16),
        vm((nb, h, 2 * HD, B), BF16), vm((nb, hs, B), BF16),
        vm((nb, 8, B), F32), vm((nb, 8, B), F32), vm((nb, h, HD, B), F32),
        vm((nb, h, 2 * HD, B), F32),
        vm((T // 2, D), BF16),
        vm((d.nx, T // 2, D), BF16), vm((d.nx, T // 2, D), BF16),
        vm((2, T // 2, D), BF16), vm((2, T // 2, D), BF16),
    ]
    widths = (wide_a, F, F)
    scratch += [vm((2, nz, HR, w), BF16) for w in widths[1:]]
    scratch += [vm((nz, HR, w), BF16) for w in widths]
    scratch += [vm((nz - 1, HR, w), BF16) for w in widths]
    scratch += [vm((nc, HR, w), BF16) for w in widths]
    scratch += [vm((8, W), F32), vm((nz * nc, 8, W), F32), vm((d.nt, 8, W), F32)]
    scratch += [pltpu.SemaphoreType.DMA((d.n_copies,)), pltpu.SemaphoreType.DMA((d.n_copies,))]

    def kernel(*refs):
        layer_kernel(d, *refs)

    out, ig, ga, gb, gc, small = pl.pallas_call(
        kernel,
        out_shape=(
            jax.ShapeDtypeStruct((T, D), F32),
            jax.ShapeDtypeStruct((T, D), F32),
            jax.ShapeDtypeStruct((R, wide_a), F32),
            jax.ShapeDtypeStruct((R, F), F32),
            jax.ShapeDtypeStruct((R, F), F32),
            jax.ShapeDtypeStruct((8, W), F32),
        ),
        in_specs=[pl.BlockSpec(memory_space=vm)] * len(args),
        out_specs=[pl.BlockSpec(memory_space=vm)] * 6,
        scratch_shapes=scratch,
        compiler_params=pltpu.CompilerParams(
            collective_id=0, has_side_effects=True, vmem_limit_bytes=VMEM_BYTES
        ),
    )(*args)
    return (
        out,
        ig,
        small[0, :D],
        small[1, :D],
        small[2, :D],
        small[3, :D],
        ga[:, : 3 * hs].reshape(R, 3, hs),
        small[6, : 3 * hs].reshape(3, hs),
        ga[:, 3 * hs :].T,
        small[4, :D],
        gb,
        small[5, :F],
        gc.T,
        small[4, :D],
    )


def solution(mesh):
    in_specs = (
        P(("fsdp", "ctx"), None),
        P("fsdp"),
        P(("fsdp", "ctx")),
        P(),
        P(),
        P(),
        P(),
        P("fsdp", None, "tp"),
        P(None, "tp"),
        P("tp", "fsdp"),
        P(),
        P("fsdp", "tp"),
        P("tp"),
        P("tp", "fsdp"),
        P(),
        P(("fsdp", "ctx"), None),
    )
    out_specs = (
        P(("fsdp", "ctx"), None),
        P(("fsdp", "ctx"), None),
        P(),
        P(),
        P(),
        P(),
        P("fsdp", None, "tp"),
        P(None, "tp"),
        P("tp", "fsdp"),
        P(),
        P("fsdp", "tp"),
        P("tp"),
        P("tp", "fsdp"),
        P(),
    )

    def step(*args):
        return body(mesh, *args)

    return jax.shard_map(step, mesh=mesh, in_specs=in_specs, out_specs=out_specs, check_vma=False)
```

profile of v0, /device:TPU:27, one launch (start us, length us, event | category | flops | bytes accessed | tf_op | source)
XLA Modules:
  0.0 186.2 jit_solution(9723012769479040847)
XLA Ops:
  0.7 0.7 convert_element_type.3
  1.4 0.8 multiply_sine_fusion
  2.2 0.7 stack.21
  2.9 0.7 stack.22
  3.6 0.7 stack.23
  4.3 0.7 stack.24
  4.9 0.7 add.3
  5.7 0.6 stack.26.refs_5_
  6.3 1.6 reshape.57.refs_6_
  7.9 1.3 reshape.54.refs_7_
  9.2 1.0 copy.34
  10.2 1.1 copy.33
  11.3 0.2 copy.35
  11.5 0.8 pad_maximum_fusion.refs_8_
  12.3 156.0 %shard_map.254 = (f32[1024,768]{1,0:T(8,128)}, f32[1024,768]{1,0:T(8,128)}, f32[192,768]{1,0:T(8,128)}, f32[192,768]{1,0:T(8,128)}, f32[192,768]{1,0:T(8,128)}, /*index=5*/f32[8,768]{1,0:T(8,128)}) custom-call(bf16[1024,768]{1,0:T(8,128)(2,1)} %refs_0_.1, f32[1024,768]{1,0:T(8,128)} %refs_1_.1, s32[2,1,512]{2,1,0:T(1,128)} %bitcast.13, ...), custom_call_target="tpu_custom_call" | custom-call | tf_op jit(solution)/shard_map/pallas_call | solution.py:678
  168.3 0.0 copy-start.1
  168.3 1.6 slice_reduce_fusion
  170.0 0.0 copy-start.4
  170.0 1.8 slice.32
  171.8 2.1 %copy.37 = f32[192,576]{0,1:T(8,128)} copy(f32[192,576]{1,0:T(8,128)} %slice.32) | data formatting | bytes 884736 | tf_op jit(solution)/shard_map/slice | solution.py:702
  173.9 2.1 %copy.38 = f32[192,3,192]{2,0,1:T(8,128)} copy(f32[192,3,192]{0,2,1:T(8,128)} %bitcast.8) | data formatting | bytes 884736
  176.0 0.7 slice_reduce_fusion.6
  176.7 0.7 reshape_squeeze.3
  177.4 1.0 slice_bitcast_fusion
  178.5 0.8 copy.39
  179.3 0.6 copy.45
  179.8 0.0 copy-done.1
  179.8 0.0 copy-start
  179.8 1.7 copy.46
  181.5 0.0 copy-done.4
  181.5 1.4 copy-done
  182.9 0.0 copy-start.3
  182.9 0.0 copy-start.2
  182.9 1.7 copy.47
  184.5 0.0 copy-done.3
  184.5 0.8 copy.48
  185.4 0.0 copy-done.2
  185.4 0.8 copy.49
  (3 shorter events, 0.0 us)
Async XLA Ops:
  168.3 11.5 %copy-start.1 = (f32[1024,768]{1,0:T(8,128)S(1)}, f32[1024,768]{1,0:T(8,128)}, u32[]{:S(2)}) copy-start(f32[1024,768]{1,0:T(8,128)} %get-tuple-element.104) | copy-start | bytes 9437188
  170.0 11.6 %copy-start.4 = (f32[768]{0:T(1024)}, f32[768]{0:T(1024)S(1)}, u32[]{:S(2)}) copy-start(f32[768]{0:T(1024)S(1)} %get-tuple-element.113) | copy-start | bytes 9220
  179.8 3.0 %copy-start = (f32[1024,768]{1,0:T(8,128)S(1)}, f32[1024,768]{1,0:T(8,128)}, u32[]{:S(2)}) copy-start(f32[1024,768]{1,0:T(8,128)} %get-tuple-element.105) | copy-start | bytes 9437188
  182.9 1.7 copy-start.3
  182.9 2.5 %copy-start.2 = (f32[192,768]{1,0:T(8,128)S(1)}, f32[192,768]{1,0:T(8,128)}, u32[]{:S(2)}) copy-start(f32[192,768]{1,0:T(8,128)} %get-tuple-element.25) | copy-start | bytes 1769476
where the time goes:
time: 187 us; the launch traced here: 186 us
  Pallas kernels  156 us (83%)
  local copies, waits for them, and re-layouts  26.4 us (14%)
  other arithmetic  3.05 us (2%)
    pallas_call x1, Pallas kernels, body(): pl.pallas_call(kernel, out_shape=(jax.ShapeDtypeStruct((T, D), F32), jax....  156 us
    unnamed x19, local copies, waits for them, and re-layouts  12 us
    slice x2, local copies, waits for them, and re-layouts, body(): ga[:, :3 * hs].reshape(R, 3, hs)  3.9 us

commit v1 on v0

--- a/solution.py
+++ b/solution.py
@@ -1,3 +1,5 @@
+import math
+
 import jax
 import jax.numpy as jnp
 from jax import lax
@@ -74,15 +76,15 @@
 
 
 def layer_kernel(d, *refs):
-    (x, og, pos, cosr, sinr, vec, bq, bf1, wa, wb, wc) = refs[:11]
-    (out, ig, ga, gb_out, gc_out, sm_out) = refs[11:17]
+    (x, og, pos_in, gain1, shift1, gain2, shift2, bq_in, bf_in, wq_in, wo_in, wb, wc) = refs[:13]
+    (u_out, e_out, ga_out, gb_out, gc_out, sm_out) = refs[13:19]
     (
         WA, WB, WC, WT, h1, h2, tA, gb, gbT, mean_s, inv_s, act, dpre,
         qz, kv, kvn, doz, ctxT, lse, dlt, dq, dkv,
         ra, chU, chE, finU, finE,
         ggB, ggC, r1A, r1B, r1C, r2A, r2B, r2C, f3A, f3B, f3C,
-        sm, smr, smt, send, recv,
-    ) = refs[17:]
+        sm, smr, smt, out, ig, wa, cosr, sinr, pos, send, recv, local,
+    ) = refs[19:]
     ub, ggA = h2, ggB
     T, D, hs, F = d.tok, d.width, d.span, d.hidden
     nz, nc, nt, nx = d.nz, d.nc, d.nt, d.nx
@@ -118,6 +120,7 @@
         return pl.ds(pl.multiple_of(src * R + part * HR, HR), HR)
 
     gathers = []
+    wa[...] = jnp.concatenate([wq_in[0], wq_in[1], wq_in[2], jnp.transpose(wo_in[...])], 1)
     for shard, full in ((wa, WA), (wb, WB), (wc, WC)):
         first = [
             net.copy(shard.at[half_here], full.at[rows_of(z)], (turn(z, r, nz), c, t))
@@ -141,7 +144,19 @@
             two.wait_recv()
 
     sm[...] = jnp.zeros_like(sm)
-    g1, b1, g2, b2 = vec[0:1, :], vec[1:2, :], vec[2:3, :], vec[3:4, :]
+    g1, b1, g2, b2 = [one[...].reshape(1, D) for one in (gain1, shift1, gain2, shift2)]
+    bf1 = bf_in[...].reshape(1, F)
+    positions = pos_in[...].reshape(1, T)
+    exponent = lax.broadcasted_iota(jnp.int32, (HALF, 1), 0).astype(F32) * (-2.0 / ROT)
+    freqs = jnp.exp(exponent * math.log(10000.0))
+    for i in range(nb):
+        pos[i] = positions[:, i * B : (i + 1) * B]
+        angle = pos[i].astype(F32) * freqs
+        cosr[i] = jnp.cos(angle)
+        sinr[i] = jnp.sin(angle)
+    bq = jnp.concatenate(
+        [jnp.transpose(jnp.broadcast_to(bq_in[j : j + 1, :], (128, hs)))[:, :1] for j in range(3)], 0
+    )
 
     def norm_tile(i, carry):
         rows = tile_rows(i, TB)
@@ -173,7 +188,7 @@
     WT[...] = jnp.transpose(WA[...])
 
     for i in range(nb):
-        proj = mm_nt(WT[: 3 * hs, :], h1[i * B : (i + 1) * B, :]) + bq[...]
+        proj = mm_nt(WT[: 3 * hs, :], h1[i * B : (i + 1) * B, :]) + bq
         cb, sb = cosr[i], sinr[i]
 
         def rotated(tensor):
@@ -219,7 +234,7 @@
 
     def mlp_tile(i, carry):
         rows = tile_rows(i, TB)
-        pre = mm(h2[rows, :], WB[...]) + bf1[...]
+        pre = mm(h2[rows, :], WB[...]) + bf1
         cdf = 0.5 * (1.0 + lax.erf(pre * INV_ROOT_TWO))
         density = jnp.exp(-0.5 * pre * pre) * INV_ROOT_TWO_PI
         actb = (pre * cdf).astype(BF16)
@@ -242,8 +257,9 @@
             gg[k % 2, z0 + k // 2] = value[k * HR : (k + 1) * HR].astype(BF16)
 
     class Reduce:
-        def __init__(self, gg, r1, r2, f3, final):
-            self.gg, self.r1, self.r2, self.f3, self.final = gg, r1, r2, f3, final
+        def __init__(self, i, gg, r1, r2, f3, final):
+            self.gg, self.r1, self.r2, self.f3 = gg, r1, r2, f3
+            self.put = pltpu.make_async_copy(f3, final, local.at[i])
             self.a = net.copy(gg.at[other], r1, (z, pair, t))
             self.b = [
                 net.copy(gg.at[part, turn(z, r, nz)], r2.at[r - 1], (turn(z, r, nz), c, t))
@@ -273,19 +289,15 @@
         def four(self):
             for one in self.c:
                 one.wait_recv()
-            for p in range(2):
-                total = self.f3[p].astype(F32)
-                for j in range(1, nc // 2):
-                    total += self.f3[2 * j + p].astype(F32)
-                self.final[p * HR : (p + 1) * HR, :] = total
+            self.put.start()
 
         def drain(self):
             for one in [self.a, *self.b, *self.c]:
                 one.wait_send()
 
-    redB = Reduce(ggB, r1B, r2B, f3B, gb_out)
-    redC = Reduce(ggC, r1C, r2C, f3C, gc_out)
-    redA = Reduce(ggA, r1A, r2A, f3A, ga)
+    redB = Reduce(0, ggB, r1B, r2B, f3B, gb_out)
+    redC = Reduce(1, ggC, r1C, r2C, f3C, gc_out)
+    redA = Reduce(2, ggA, r1A, r2A, f3A, ga_out)
 
     for z0 in range(0, nz, 2):
         store_grad(ggB, mm(tA[z0 * R : (z0 + 2) * R, :], dpre[...]), z0)
@@ -539,14 +551,8 @@
     join_e.two()
     redA.two()
 
-    def out_tile(i, carry):
-        rows = tile_rows(i, TB)
-        per = T // 2 // TB
-        total = finU[i // per, tile_rows(lax.rem(i, per), TB), :].astype(F32)
-        out[rows, :] = x[rows, :].astype(F32) + total + vec[4:5, :]
-        return carry
-
-    lax.fori_loop(0, T // TB, out_tile, 0)
+    put_u = pltpu.make_async_copy(finU, u_out, local.at[3])
+    put_u.start()
     redB.four()
     redC.four()
 
@@ -569,19 +575,8 @@
     sm_out[...] = jnp.concatenate([tops, tot[4:8, :]], 0)
     join_e.four()
 
-    def in_tile(i, carry):
-        rows = tile_rows(i, TB)
-        per = T // 2 // TB
-        e = finE[i // per, tile_rows(lax.rem(i, per), TB), :].astype(F32)
-        normed = normed_of(rows)
-        ig[rows, :] = og[rows, :] + inv_s[rows, :] * (
-            e
-            - jnp.mean(e, -1, keepdims=True)
-            - normed * jnp.mean(e * normed, -1, keepdims=True)
-        )
-        return carry
-
-    lax.fori_loop(0, T // TB, in_tile, 0)
+    put_e = pltpu.make_async_copy(finE, e_out, local.at[4])
+    put_e.start()
     redA.four()
 
     for first, second in gathers:
@@ -608,6 +603,8 @@
     join_e.drain()
     for one in [*small_a, *small_b]:
         one.wait_send()
+    for one in (redA.put, redB.put, redC.put, put_u, put_e):
+        one.wait()
     assert net.used == d.n_copies
 
 
@@ -633,20 +630,19 @@
     d = Dims(mesh, layer_input.shape[0], layer_input.shape[1], b_qkv.shape[1], b_fc1.shape[0])
     T, D, hs, F, B, nb = d.tok, d.width, d.span, d.hidden, d.blk, d.nb
     R, HR, nz, nc = d.rows, d.half, d.nz, d.nc
-    freqs = 10000.0 ** (-(jnp.arange(HALF, dtype=F32) * 2.0) / ROT)
-    angles = positions.astype(F32).reshape(nb, 1, B) * freqs[None, :, None]
-    vec = jnp.stack([ln1_gain, ln1_bias, ln2_gain, ln2_bias, b_out + b_fc2] + [ln1_gain] * 3)
     wide_a = 4 * hs
     args = (
         layer_input,
         out_grad,
-        positions.reshape(nb, 1, B),
-        jnp.cos(angles),
-        jnp.sin(angles),
-        vec,
-        b_qkv.reshape(3 * hs, 1),
-        b_fc1.reshape(1, F),
-        jnp.concatenate([w_qkv.reshape(R, 3 * hs), w_out.T], 1),
+        positions,
+        ln1_gain,
+        ln1_bias,
+        ln2_gain,
+        ln2_bias,
+        b_qkv,
+        b_fc1,
+        jnp.transpose(w_qkv, (1, 0, 2)),
+        w_out,
         w_fc1,
         w_fc2.T,
     )
@@ -670,44 +666,95 @@
     scratch += [vm((nz - 1, HR, w), BF16) for w in widths]
     scratch += [vm((nc, HR, w), BF16) for w in widths]
     scratch += [vm((8, W), F32), vm((nz * nc, 8, W), F32), vm((d.nt, 8, W), F32)]
-    scratch += [pltpu.SemaphoreType.DMA((d.n_copies,)), pltpu.SemaphoreType.DMA((d.n_copies,))]
+    scratch += [vm((T, D), F32), vm((T, D), F32), vm((R, wide_a), BF16)]
+    scratch += [vm((nb, HALF, B), F32), vm((nb, HALF, B), F32), vm((nb, 1, B), jnp.int32)]
+    scratch += [pltpu.SemaphoreType.DMA((n,)) for n in (d.n_copies, d.n_copies, 5)]
 
     def kernel(*refs):
         layer_kernel(d, *refs)
 
-    out, ig, ga, gb, gc, small = pl.pallas_call(
+    fin = jax.ShapeDtypeStruct((2, T // 2, D), BF16)
+    sums = [jax.ShapeDtypeStruct((nc, HR, w), BF16) for w in widths]
+    in_hbm = pl.BlockSpec(memory_space=pl.ANY)
+    joined, joined_e, *owned, small = pl.pallas_call(
         kernel,
-        out_shape=(
-            jax.ShapeDtypeStruct((T, D), F32),
-            jax.ShapeDtypeStruct((T, D), F32),
-            jax.ShapeDtypeStruct((R, wide_a), F32),
-            jax.ShapeDtypeStruct((R, F), F32),
-            jax.ShapeDtypeStruct((R, F), F32),
-            jax.ShapeDtypeStruct((8, W), F32),
-        ),
+        out_shape=(fin, fin, *sums, jax.ShapeDtypeStruct((8, W), F32)),
         in_specs=[pl.BlockSpec(memory_space=vm)] * len(args),
-        out_specs=[pl.BlockSpec(memory_space=vm)] * 6,
+        out_specs=[in_hbm] * 5 + [pl.BlockSpec(memory_space=vm)],
         scratch_shapes=scratch,
         compiler_params=pltpu.CompilerParams(
             collective_id=0, has_side_effects=True, vmem_limit_bytes=VMEM_BYTES
         ),
     )(*args)
-    return (
-        out,
-        ig,
-        small[0, :D],
-        small[1, :D],
-        small[2, :D],
-        small[3, :D],
-        ga[:, : 3 * hs].reshape(R, 3, hs),
-        small[6, : 3 * hs].reshape(3, hs),
-        ga[:, 3 * hs :].T,
-        small[4, :D],
-        gb,
-        small[5, :F],
-        gc.T,
-        small[4, :D],
+
+    TB = d.tile
+
+    def tiles():
+        return pl.BlockSpec((TB, D), lambda i: (i, 0))
+
+    def whole(shape):
+        return pl.BlockSpec(shape, lambda i: (0,) * len(shape))
+
+    outs = [
+        ((T, D), True), ((T, D), True), ((D,), False), ((D,), False), ((D,), False), ((D,), False),
+        ((3, R, hs), False), ((3, hs), False), ((hs, R), False), ((D,), False), ((R, F), False),
+        ((F,), False), ((R, F), False), ((D,), False),
+    ]
+    results = pl.pallas_call(
+        lambda *refs: finish_kernel(d, *refs),
+        grid=(T // TB,),
+        out_shape=[jax.ShapeDtypeStruct(shape, F32) for shape, _ in outs],
+        in_specs=[tiles(), tiles(), tiles(), tiles()]
+        + [whole(o.shape) for o in owned]
+        + [whole((8, W)), whole((D,)), whole((D,))],
+        out_specs=[tiles() if tiled else whole(shape) for shape, tiled in outs],
+        compiler_params=pltpu.CompilerParams(vmem_limit_bytes=VMEM_BYTES),
+    )(
+        layer_input, out_grad, joined.reshape(T, D), joined_e.reshape(T, D), *owned, small, b_out, b_fc2
     )
+    results = list(results)
+    results[6] = jnp.transpose(results[6], (1, 0, 2))
+    results[12] = results[12].T
+    return tuple(results)
+
+
+def finish_kernel(d, x, og, u, e, fa, fb, fc, small, bo, bf2, *outs):
+    out, ig, o_g1, o_b1, o_g2, o_b2, o_qkv, o_bqkv, o_wo, o_bo, o_fc1, o_bf1, o_fc2, o_bf2 = outs
+    D, hs, F, HR = d.width, d.span, d.hidden, d.half
+    xf = x[...].astype(F32)
+    out[...] = xf + u[...].astype(F32) + (bo[...] + bf2[...]).reshape(1, D)
+    cen = xf - jnp.mean(xf, -1, keepdims=True)
+    inv = lax.rsqrt(jnp.mean(cen * cen, -1, keepdims=True) + NORM_EPS)
+    normed = cen * inv
+    ee = e[...].astype(F32)
+    ig[...] = og[...] + inv * (
+        ee - jnp.mean(ee, -1, keepdims=True) - normed * jnp.mean(ee * normed, -1, keepdims=True)
+    )
+
+    def summed(slots, p):
+        total = slots[p].astype(F32)
+        for j in range(1, d.nc // 2):
+            total += slots[2 * j + p].astype(F32)
+        return total
+
+    @pl.when(pl.program_id(0) == 0)
+    def _():
+        for p in range(2):
+            rows = slice(p * HR, (p + 1) * HR)
+            half_a = summed(fa, p)
+            for j in range(3):
+                o_qkv[j, rows, :] = half_a[:, j * hs : (j + 1) * hs]
+            o_fc1[rows, :] = summed(fb, p)
+            o_fc2[rows, :] = summed(fc, p)
+        whole_a = jnp.concatenate([summed(fa, 0), summed(fa, 1)], 0)
+        o_wo[...] = jnp.transpose(whole_a[:, 3 * hs :])
+        for k, (o, n) in enumerate(
+            ((o_g1, D), (o_b1, D), (o_g2, D), (o_b2, D), (o_bo, D), (o_bf1, F))
+        ):
+            o[...] = small[k : k + 1, :n].reshape(n)
+        o_bf2[...] = small[4:5, :D].reshape(D)
+        for j in range(3):
+            o_bqkv[j : j + 1, :] = small[6:7, j * hs : (j + 1) * hs]
 
 
 def solution(mesh):

time: 187 us -> 163 us (0.87)
  the two profiles are of different devices: /device:TPU:27 before, /device:TPU:30 now
where the time goes in v1:
time: 163 us
  Pallas kernels  162 us (99%)
    pallas_call x1, Pallas kernels, body(): pl.pallas_call(kernel, out_shape=(fin, fin, *sums, jax.ShapeDtypeStruct((...  153 us
    pallas_call x1, Pallas kernels, body(): pl.pallas_call(lambda *refs: finish_kernel(d, *refs), grid=(T // TB,), ou...  8.45 us

profile of v1, /device:TPU:30, one launch (start us, length us, event | category | flops | bytes accessed | tf_op | source)
XLA Modules:
  0.0 162.6 jit_solution(13024229469607026034)
XLA Ops:
  0.6 153.3 %shard_map.254 = (bf16[2,512,768]{2,1,0:T(8,128)(2,1)}, bf16[2,512,768]{2,1,0:T(8,128)(2,1)}, bf16[2,96,768]{2,1,0:T(8,128)(2,1)}, bf16[2,96,768]{2,1,0:T(8,128)...) custom-call(bf16[1024,768]{1,0:T(8,128)(2,1)} %refs_0_.3, f32[1024,768]{1,0:T(8,128)} %refs_1_.3, s32[1024]{0:T(1024)} %refs_2_.1, ...), custom_call_target="tpu_custom_call" | custom-call | tf_op jit(solution)/shard_map/pallas_call | solution.py:679
  154.0 8.5 %shard_map.255 = (f32[1024,768]{1,0:T(8,128)}, f32[1024,768]{1,0:T(8,128)}, f32[768]{0:T(1024)}, f32[768]{0:T(1024)}, f32[768]{0:T(1024)}, /*index=5*/f32[768]{0...) custom-call(bf16[1024,768]{1,0:T(8,128)(2,1)} %refs_0_.3, ...), custom_call_target="tpu_custom_call" | custom-call | tf_op jit(solution)/shard_map/pallas_call | solution.py:703

commit v2 on v1

--- a/solution.py
+++ b/solution.py
@@ -49,10 +49,12 @@
         self.wide = max(width, hidden, 3 * span)
         nz, nc, nx = self.nz, self.nc, self.nx
         self.n_copies = (
-            3 * 2 * (nz - 1)
+            3 * 4 * (nz - 1)
             + 2 * (nc - 1)
             + 2 * (nx + 1)
-            + 3 * (1 + (nz - 1) + (nc - 1))
+            + 2 * (nz + (nz - 1) + (nc - 1))
+            + (nz - 1)
+            + (nc - 1)
             + (nz * nc - 1)
             + (self.nt - 1)
         )
@@ -82,10 +84,12 @@
         WA, WB, WC, WT, h1, h2, tA, gb, gbT, mean_s, inv_s, act, dpre,
         qz, kv, kvn, doz, ctxT, lse, dlt, dq, dkv,
         ra, chU, chE, finU, finE,
-        ggB, ggC, r1A, r1B, r1C, r2A, r2B, r2C, f3A, f3B, f3C,
+        ggA, ggB, ggC, r1A, r1B, r2A, r2B, r2C, f3A, f3B, f3C,
         sm, smr, smt, out, ig, wa, cosr, sinr, pos, send, recv, local,
     ) = refs[19:]
-    ub, ggA = h2, ggB
+    ub = h2
+    if not d.keep:
+        ggA = ggB
     T, D, hs, F = d.tok, d.width, d.span, d.hidden
     nz, nc, nt, nx = d.nz, d.nc, d.nt, d.nx
     heads, B, nb, R, HR, TB = d.heads, d.blk, d.nb, d.rows, d.half, d.tile
@@ -119,29 +123,55 @@
     def rows_of(src):
         return pl.ds(pl.multiple_of(src * R + part * HR, HR), HR)
 
-    gathers = []
     wa[...] = jnp.concatenate([wq_in[0], wq_in[1], wq_in[2], jnp.transpose(wo_in[...])], 1)
-    for shard, full in ((wa, WA), (wb, WB), (wc, WC)):
-        first = [
-            net.copy(shard.at[half_here], full.at[rows_of(z)], (turn(z, r, nz), c, t))
-            for r in range(1, nz)
-        ]
-        second = []
-        for r in range(1, nz):
-            src = turn(z, nz - r, nz)
-            second.append(net.copy(full.at[rows_of(src)], full.at[rows_of(src)], (z, pair, t)))
-        gathers.append((first, second))
-        for one in first:
-            one.start()
-
-    def relay(i):
-        for one, two in zip(*gathers[i]):
-            one.wait_recv()
-            two.start()
-
-    def gathered(i):
-        for two in gathers[i][1]:
-            two.wait_recv()
+
+    class Gather:
+        def __init__(self, shard, full):
+            self.moves = []
+            for step in (1, -1):
+                to = jnp.clip(z + step, 0, nz - 1)
+                has_next = (z + 1 < nz) if step == 1 else (z > 0)
+                for k in range(1, nz):
+                    sent, come = z - step * (k - 1), z - step * k
+                    inside = (come >= 0) if step == 1 else (come < nz)
+                    has_sent = (sent >= 0) if step == 1 else (sent < nz)
+                    at = rows_of(jnp.clip(sent, 0, nz - 1))
+                    src = shard.at[half_here] if k == 1 else full.at[at]
+                    hop = net.copy(src, full.at[at], (to, c, t))
+                    got = rows_of(jnp.clip(come, 0, nz - 1))
+                    side = net.copy(full.at[got], full.at[got], (z, pair, t))
+                    self.moves.append((k, hop, side, inside, has_next, has_sent & has_next))
+
+        def start(self):
+            for k, hop, side, inside, has_next, sends in self.moves:
+                if k == 1:
+                    pl.when(sends)(hop.start)
+
+        def pump(self, k):
+            for i, (kk, hop, side, inside, has_next, sends) in enumerate(self.moves):
+                if kk == k:
+                    onward = self.moves[i + 1] if k + 1 < nz else None
+
+                    @pl.when(inside)
+                    def _():
+                        hop.wait_recv()
+                        if onward is not None:
+                            pl.when(has_next)(onward[1].start)
+                        side.start()
+
+        def done(self):
+            for k, hop, side, inside, has_next, sends in self.moves:
+                pl.when(inside)(side.wait_recv)
+
+        def drain(self):
+            for k, hop, side, inside, has_next, sends in self.moves:
+                pl.when(sends)(hop.wait_send)
+                pl.when(inside)(side.wait_send)
+
+    gather_a, gather_b, gather_c = [
+        Gather(shard, full) for shard, full in ((wa, WA), (wb, WB), (wc, WC))
+    ]
+    gather_a.start()
 
     sm[...] = jnp.zeros_like(sm)
     g1, b1, g2, b2 = [one[...].reshape(1, D) for one in (gain1, shift1, gain2, shift2)]
@@ -183,9 +213,13 @@
         gbT[i] = jnp.transpose(gb[i * B : (i + 1) * B, :])
         tA[:, i * B : (i + 1) * B] = jnp.transpose(h2[i * B : (i + 1) * B, :])
 
-    relay(0)
-    gathered(0)
+    for k in range(1, nz):
+        gather_a.pump(k)
+        if k == max(1, nz - 2):
+            gather_b.start()
+    gather_a.done()
     WT[...] = jnp.transpose(WA[...])
+    gather_b.pump(1)
 
     for i in range(nb):
         proj = mm_nt(WT[: 3 * hs, :], h1[i * B : (i + 1) * B, :]) + bq
@@ -206,18 +240,16 @@
             if d.keep:
                 kvn[own, h] = jnp.transpose(both)
 
+    for k in range(2, nz):
+        gather_b.pump(k)
+        if k == max(2, nz - 2):
+            gather_c.start()
     own_blocks = pl.ds(c * nb, nb)
     kv_out = [
         net.copy(kv.at[own_blocks], kv.at[own_blocks], (z, turn(c, r, nc), t))
         for r in range(1, nc)
     ]
-    for r, one in enumerate(kv_out, 1):
-
-        @pl.when(c + r < nc)
-        def _(one=one):
-            one.start()
-
-    relay(1)
+    gather_c.pump(1)
 
     for i in range(nb):
         dct = mm(WT[3 * hs :, :], gbT[i]).astype(BF16)
@@ -225,9 +257,16 @@
             piece = dct[h * HD : (h + 1) * HD]
             doz[i, h] = jnp.concatenate([jnp.zeros_like(piece), piece], 0)
 
-    relay(2)
-    gathered(1)
-    gathered(2)
+    for k in range(2, nz):
+        gather_c.pump(k)
+    for r, one in enumerate(kv_out, 1):
+
+        @pl.when(c + r < nc)
+        def _(one=one):
+            one.start()
+
+    gather_b.done()
+    gather_c.done()
 
     def normed_of(rows):
         return (x[rows, :].astype(F32) - mean_s[rows, :]) * inv_s[rows, :]
@@ -260,7 +299,10 @@
         def __init__(self, i, gg, r1, r2, f3, final):
             self.gg, self.r1, self.r2, self.f3 = gg, r1, r2, f3
             self.put = pltpu.make_async_copy(f3, final, local.at[i])
-            self.a = net.copy(gg.at[other], r1, (z, pair, t))
+            self.a = [
+                net.copy(gg.at[other, turn(z, r, nz)], r1.at[turn(z, r, nz)], (z, pair, t))
+                for r in range(nz)
+            ]
             self.b = [
                 net.copy(gg.at[part, turn(z, r, nz)], r2.at[r - 1], (turn(z, r, nz), c, t))
                 for r in range(1, nz)
@@ -268,16 +310,18 @@
             self.c = [net.copy(f3.at[c], f3.at[c], (z, turn(c, r, nc), t)) for r in range(1, nc)]
 
         def one(self):
-            self.a.start()
+            for one in [*self.a[1:], self.a[0]]:
+                one.start()
 
         def two(self):
-            self.a.wait_recv()
             for r in range(1, nz):
+                self.a[r].wait_recv()
                 zz = turn(z, r, nz)
                 self.gg[part, zz] = (self.gg[part, zz].astype(F32) + self.r1[zz].astype(F32)).astype(BF16)
                 self.b[r - 1].start()
 
         def three(self):
+            self.a[0].wait_recv()
             total = self.gg[part, z].astype(F32) + self.r1[z].astype(F32)
             for r in range(1, nz):
                 self.b[r - 1].wait_recv()
@@ -292,11 +336,43 @@
             self.put.start()
 
         def drain(self):
-            for one in [self.a, *self.b, *self.c]:
+            for one in [*self.a, *self.b, *self.c]:
                 one.wait_send()
 
+    class ReduceFlat:
+        def __init__(self, i, gg, r2, f3, final):
+            self.gg, self.r2, self.f3 = gg, r2, f3
+            self.put = pltpu.make_async_copy(f3, final, local.at[i])
+            self.b = [
+                net.copy(gg.at[turn(z, r, nz)], r2.at[r - 1], (turn(z, r, nz), c, t))
+                for r in range(1, nz)
+            ]
+            self.c = [net.copy(f3.at[c], f3.at[c], (z, turn(c, r, nc), t)) for r in range(1, nc)]
+
+        def one(self):
+            for one in self.b:
+                one.start()
+
+        def three(self):
+            total = self.gg[z].astype(F32)
+            for r in range(1, nz):
+                self.b[r - 1].wait_recv()
+                total += self.r2[r - 1].astype(F32)
+            self.f3[c] = total.astype(BF16)
+            for one in self.c:
+                one.start()
+
+        def four(self):
+            for one in self.c:
+                one.wait_recv()
+            self.put.start()
+
+        def drain(self):
+            for one in [*self.b, *self.c]:
+                one.wait_send()
+
     redB = Reduce(0, ggB, r1B, r2B, f3B, gb_out)
-    redC = Reduce(1, ggC, r1C, r2C, f3C, gc_out)
+    redC = ReduceFlat(1, ggC, r2C, f3C, gc_out)
     redA = Reduce(2, ggA, r1A, r2A, f3A, ga_out)
 
     for z0 in range(0, nz, 2):
@@ -307,7 +383,8 @@
         for i in range(nb):
             term = mm(gbT[i, z0 * R : (z0 + 2) * R, :], act[i * B : (i + 1) * B, :])
             value = term if value is None else value + term
-        store_grad(ggC, value, z0)
+        for k in range(2):
+            ggC[z0 + k] = value[k * R : (k + 1) * R].astype(BF16)
     redC.one()
 
     for r, one in enumerate(kv_out, 1):
@@ -421,8 +498,6 @@
                 out[rows, :] + mm(ctx_n[k * TB : (k + 1) * TB], WT[3 * hs :, :])
             ).astype(BF16)
     join_u.one()
-    redB.two()
-    redC.two()
 
     dq[...] = jnp.zeros_like(dq)
 
@@ -481,8 +556,7 @@
         return carry
 
     lax.fori_loop(0, nb, own_block, 0)
-    redB.three()
-    redC.three()
+    redB.two()
     join_u.three()
 
     for r in range(1, nc):
@@ -519,8 +593,9 @@
         term = mm(ctxT[i], gb[i * B : (i + 1) * B, :])
         grad_o = term if grad_o is None else grad_o + term
     grad_a = jnp.transpose(jnp.concatenate([grad_q.astype(BF16), grad_o.astype(BF16)], 0))
-    for one in [redB.a, *redB.b]:
-        one.wait_send()
+    if not d.keep:
+        for one in [*redB.a, *redB.b]:
+            one.wait_send()
     store_grad(ggA, grad_a, 0)
     redA.one()
     join_u.near.wait_send()
@@ -536,6 +611,7 @@
     lax.fori_loop(0, T // TB, e_tile, 0)
     join_u.four()
     join_e.one()
+    redC.three()
 
     rank = z * nc + c
     smr[rank] = sm[...]
@@ -549,6 +625,7 @@
     for one in small_a:
         one.start()
     join_e.two()
+    redB.three()
     redA.two()
 
     put_u = pltpu.make_async_copy(finU, u_out, local.at[3])
@@ -579,9 +656,8 @@
     put_e.start()
     redA.four()
 
-    for first, second in gathers:
-        for one in [*first, *second]:
-            one.wait_send()
+    for one in (gather_a, gather_b, gather_c):
+        one.drain()
     for r, one in enumerate(kv_out, 1):
 
         @pl.when(c + r < nc)
@@ -594,7 +670,7 @@
         def _(one=one):
             one.wait_send()
 
-    for one in redB.c:
+    for one in redB.c if not d.keep else [*redB.a, *redB.b, *redB.c]:
         one.wait_send()
     redA.drain()
     redC.drain()
@@ -661,10 +737,12 @@
         vm((2, T // 2, D), BF16), vm((2, T // 2, D), BF16),
     ]
     widths = (wide_a, F, F)
-    scratch += [vm((2, nz, HR, w), BF16) for w in widths[1:]]
-    scratch += [vm((nz, HR, w), BF16) for w in widths]
-    scratch += [vm((nz - 1, HR, w), BF16) for w in widths]
-    scratch += [vm((nc, HR, w), BF16) for w in widths]
+    piece = (HR, HR, R)
+    scratch += [vm((2, nz, HR, wide_a) if d.keep else (8, 128), BF16)]
+    scratch += [vm((2, nz, HR, F), BF16), vm((nz, R, F), BF16)]
+    scratch += [vm((nz, HR, w), BF16) for w in widths[:2]]
+    scratch += [vm((nz - 1, n, w), BF16) for n, w in zip(piece, widths)]
+    scratch += [vm((nc, n, w), BF16) for n, w in zip(piece, widths)]
     scratch += [vm((8, W), F32), vm((nz * nc, 8, W), F32), vm((d.nt, 8, W), F32)]
     scratch += [vm((T, D), F32), vm((T, D), F32), vm((R, wide_a), BF16)]
     scratch += [vm((nb, HALF, B), F32), vm((nb, HALF, B), F32), vm((nb, 1, B), jnp.int32)]
@@ -674,7 +752,7 @@
         layer_kernel(d, *refs)
 
     fin = jax.ShapeDtypeStruct((2, T // 2, D), BF16)
-    sums = [jax.ShapeDtypeStruct((nc, HR, w), BF16) for w in widths]
+    sums = [jax.ShapeDtypeStruct((nc, n, w), BF16) for n, w in zip(piece, widths)]
     in_hbm = pl.BlockSpec(memory_space=pl.ANY)
     joined, joined_e, *owned, small = pl.pallas_call(
         kernel,
@@ -745,7 +823,10 @@
             for j in range(3):
                 o_qkv[j, rows, :] = half_a[:, j * hs : (j + 1) * hs]
             o_fc1[rows, :] = summed(fb, p)
-            o_fc2[rows, :] = summed(fc, p)
+        total = fc[0].astype(F32)
+        for j in range(1, d.nc):
+            total += fc[j].astype(F32)
+        o_fc2[...] = total
         whole_a = jnp.concatenate([summed(fa, 0), summed(fa, 1)], 0)
         o_wo[...] = jnp.transpose(whole_a[:, 3 * hs :])
         for k, (o, n) in enumerate(

time: 163 us -> 138 us (0.85)
  the two profiles are of different devices: /device:TPU:30 before, /device:TPU:0 now
where the time goes in v2:
time: 138 us
  Pallas kernels  137 us (99%)
    pallas_call x1, Pallas kernels, body(): pl.pallas_call(kernel, out_shape=(fin, fin, *sums, jax.ShapeDtypeStruct((...  128 us
    pallas_call x1, Pallas kernels, body(): pl.pallas_call(lambda *refs: finish_kernel(d, *refs), grid=(T // TB,), ou...  8.59 us

profile of v2, /device:TPU:0, one launch (start us, length us, event | category | flops | bytes accessed | tf_op | source)
XLA Modules:
  0.0 137.8 jit_solution(15720857100494426371)
XLA Ops:
  0.6 128.4 %shard_map.254 = (bf16[2,512,768]{2,1,0:T(8,128)(2,1)}, bf16[2,512,768]{2,1,0:T(8,128)(2,1)}, bf16[2,96,768]{2,1,0:T(8,128)(2,1)}, bf16[2,96,768]{2,1,0:T(8,128)...) custom-call(bf16[1024,768]{1,0:T(8,128)(2,1)} %refs_0_.3, f32[1024,768]{1,0:T(8,128)} %refs_1_.3, s32[1024]{0:T(1024)} %refs_2_.1, ...), custom_call_target="tpu_custom_call" | custom-call | tf_op jit(solution)/shard_map/pallas_call | solution.py:757
  129.1 8.6 %shard_map.255 = (f32[1024,768]{1,0:T(8,128)}, f32[1024,768]{1,0:T(8,128)}, f32[768]{0:T(1024)}, f32[768]{0:T(1024)}, f32[768]{0:T(1024)}, /*index=5*/f32[768]{0...) custom-call(bf16[1024,768]{1,0:T(8,128)(2,1)} %refs_0_.3, ...), custom_call_target="tpu_custom_call" | custom-call | tf_op jit(solution)/shard_map/pallas_call | solution.py:781

commit v3 on v2

--- a/solution.py
+++ b/solution.py
@@ -50,9 +50,9 @@
         nz, nc, nx = self.nz, self.nc, self.nx
         self.n_copies = (
             3 * 4 * (nz - 1)
-            + 2 * (nc - 1)
-            + 2 * (nx + 1)
-            + 2 * (nz + (nz - 1) + (nc - 1))
+            + (nc - 1) * (1 + self.nb)
+            + 2 * 2 * (nx + 1)
+            + 3 * (nz + (nz - 1) + (nc - 1))
             + (nz - 1)
             + (nc - 1)
             + (nz * nc - 1)
@@ -78,18 +78,16 @@
 
 
 def layer_kernel(d, *refs):
-    (x, og, pos_in, gain1, shift1, gain2, shift2, bq_in, bf_in, wq_in, wo_in, wb, wc) = refs[:13]
-    (u_out, e_out, ga_out, gb_out, gc_out, sm_out) = refs[13:19]
+    (x_in, og_in, pos_in, gain1, shift1, gain2, shift2, bq_in, bf_in, wq_in, wo_in, wb, wc) = refs[:13]
+    (u_out, e_out, ga_out, gb_out, gc_out, gk_out, sm_out) = refs[13:20]
     (
         WA, WB, WC, WT, h1, h2, tA, gb, gbT, mean_s, inv_s, act, dpre,
         qz, kv, kvn, doz, ctxT, lse, dlt, dq, dkv,
         ra, chU, chE, finU, finE,
-        ggA, ggB, ggC, r1A, r1B, r2A, r2B, r2C, f3A, f3B, f3C,
-        sm, smr, smt, out, ig, wa, cosr, sinr, pos, send, recv, local,
-    ) = refs[19:]
+        ggA, ggB, ggC, ggK, r1A, r1B, r1K, r2A, r2B, r2C, r2K, f3A, f3B, f3C, f3K,
+        sm, smr, smt, out, ig, wa, cosr, sinr, pos, x, send, recv, local,
+    ) = refs[20:]
     ub = h2
-    if not d.keep:
-        ggA = ggB
     T, D, hs, F = d.tok, d.width, d.span, d.hidden
     nz, nc, nt, nx = d.nz, d.nc, d.nt, d.nx
     heads, B, nb, R, HR, TB = d.heads, d.blk, d.nb, d.rows, d.half, d.tile
@@ -106,6 +104,11 @@
     def turn(value, step, size):
         return lax.rem(value + step, size)
 
+    load_x = pltpu.make_async_copy(x_in, x, local.at[6])
+    load_og = pltpu.make_async_copy(og_in, out, local.at[7])
+    load_x.start()
+    load_og.start()
+
     barrier = pltpu.get_barrier_semaphore()
     talks = []
     for rz in range(nz):
@@ -123,7 +126,7 @@
     def rows_of(src):
         return pl.ds(pl.multiple_of(src * R + part * HR, HR), HR)
 
-    wa[...] = jnp.concatenate([wq_in[0], wq_in[1], wq_in[2], jnp.transpose(wo_in[...])], 1)
+    wa[...] = jnp.concatenate([wq_in[0], jnp.transpose(wo_in[...]), wq_in[1], wq_in[2]], 1)
 
     class Gather:
         def __init__(self, shard, full):
@@ -199,11 +202,13 @@
         inv_s[rows, :] = inv
         h1[rows, :] = (normed * g1 + b1).astype(BF16)
         h2[rows, :] = (normed * g2 + b2).astype(BF16)
-        grad = og[rows, :]
+        grad = out[rows, :]
         gb[rows, :] = grad.astype(BF16)
         sm[4:5, :D] += jnp.sum(grad, 0, keepdims=True)
         return carry
 
+    load_x.wait()
+    load_og.wait()
     lax.fori_loop(0, T // TB, norm_tile, 0)
     own_rows = pl.ds(pl.multiple_of(z * R, R), R)
     WA[own_rows, :] = wa[...]
@@ -218,11 +223,13 @@
         if k == max(1, nz - 2):
             gather_b.start()
     gather_a.done()
+    gather_b.pump(1)
+    gather_c.start()
     WT[...] = jnp.transpose(WA[...])
-    gather_b.pump(1)
 
     for i in range(nb):
-        proj = mm_nt(WT[: 3 * hs, :], h1[i * B : (i + 1) * B, :]) + bq
+        hidden = h1[i * B : (i + 1) * B, :]
+        proj = jnp.concatenate([mm_nt(WT[:hs, :], hidden), mm_nt(WT[2 * hs :, :], hidden)], 0) + bq
         cb, sb = cosr[i], sinr[i]
 
         def rotated(tensor):
@@ -239,11 +246,11 @@
             kv[own, h] = both
             if d.keep:
                 kvn[own, h] = jnp.transpose(both)
-
-    for k in range(2, nz):
+        if i == 0 and nb > 1:
+            gather_b.pump(2)
+
+    for k in range(2 + (nb > 1), nz):
         gather_b.pump(k)
-        if k == max(2, nz - 2):
-            gather_c.start()
     own_blocks = pl.ds(c * nb, nb)
     kv_out = [
         net.copy(kv.at[own_blocks], kv.at[own_blocks], (z, turn(c, r, nc), t))
@@ -252,7 +259,7 @@
     gather_c.pump(1)
 
     for i in range(nb):
-        dct = mm(WT[3 * hs :, :], gbT[i]).astype(BF16)
+        dct = mm(WT[hs : 2 * hs, :], gbT[i]).astype(BF16)
         for h in range(heads):
             piece = dct[h * HD : (h + 1) * HD]
             doz[i, h] = jnp.concatenate([jnp.zeros_like(piece), piece], 0)
@@ -374,6 +381,7 @@
     redB = Reduce(0, ggB, r1B, r2B, f3B, gb_out)
     redC = ReduceFlat(1, ggC, r2C, f3C, gc_out)
     redA = Reduce(2, ggA, r1A, r2A, f3A, ga_out)
+    redK = Reduce(5, ggK, r1K, r2K, f3K, gk_out)
 
     for z0 in range(0, nz, 2):
         store_grad(ggB, mm(tA[z0 * R : (z0 + 2) * R, :], dpre[...]), z0)
@@ -387,21 +395,6 @@
             ggC[z0 + k] = value[k * R : (k + 1) * R].astype(BF16)
     redC.one()
 
-    for r, one in enumerate(kv_out, 1):
-
-        @pl.when(c >= r)
-        def _(r=r, one=one):
-            one.wait_recv()
-
-            def flip(j, carry):
-                at = (c - r) * nb + j
-                for h in range(heads):
-                    kvn[at, h] = jnp.transpose(kv[at, h])
-                return carry
-
-            if d.keep:
-                lax.fori_loop(0, nb, flip, 0)
-
     def natural(at, h):
         return kvn[at, h] if d.keep else jnp.transpose(kv[at, h])
 
@@ -410,7 +403,7 @@
         key_at = at * B + lax.broadcasted_iota(jnp.int32, (B, 1), 0)
         return (key_at <= query_at) & (key_at >= query_at - pos[i])
 
-    for i in range(nb):
+    def forward(i):
         here = c * nb + i
         first_key = jnp.where(here >= d.tail, d.tail, 0)
         for h in range(heads):
@@ -443,61 +436,87 @@
                 doz[i, h, HD:].astype(F32) * ctx_h.astype(F32), 0, keepdims=True
             )
 
+    if d.keep:
+        for i in range(1, nb):
+            early = (c * nb + i >= d.tail) | (c == 0)
+            pl.when(early)(lambda i=i: forward(i))
+    for r, one in enumerate(kv_out, 1):
+
+        @pl.when(c >= r)
+        def _(r=r, one=one):
+            one.wait_recv()
+
+            def flip(j, carry):
+                at = (c - r) * nb + j
+                for h in range(heads):
+                    kvn[at, h] = jnp.transpose(kv[at, h])
+                return carry
+
+            if d.keep:
+                lax.fori_loop(0, nb, flip, 0)
+
+    for i in range(nb):
+        if d.keep and i:
+            late = (c * nb + i < d.tail) & (c > 0)
+            pl.when(late)(lambda i=i: forward(i))
+        else:
+            forward(i)
+
+    chunks = 2
+    CH = T // 2 // chunks
+
+    def half_rows(which, k):
+        return pl.ds(pl.multiple_of(which * (T // 2) + k * CH, CH), CH)
+
     class Join:
         def __init__(self, ra, ch, fin):
             self.ra, self.ch, self.fin = ra, ch, fin
-            self.near = net.copy(
-                ub.at[pl.ds(pl.multiple_of((1 - core) * (T // 2), T // 2), T // 2)], ra, (z, c, mate)
-            )
-            self.far = [
-                net.copy(ch.at[xg], ch.at[xg], (z, c, turn(xg, r, nx) * 2 + core))
-                for r in range(1, nx)
-            ]
-            self.back = net.copy(fin.at[core], fin.at[core], (z, c, mate))
-
-        def one(self):
-            self.near.start()
+            self.near, self.far, self.back = [], [], []
+            for k in range(chunks):
+                tile = pl.ds(k * CH, CH)
+                self.near.append(net.copy(ub.at[half_rows(1 - core, k)], ra.at[tile], (z, c, mate)))
+                self.far.append(
+                    [
+                        net.copy(ch.at[xg, tile], ch.at[xg, tile], (z, c, turn(xg, r, nx) * 2 + core))
+                        for r in range(1, nx)
+                    ]
+                )
+                self.back.append(net.copy(fin.at[core, tile], fin.at[core, tile], (z, c, mate)))
 
         def two(self):
-            self.near.wait_recv()
-            for k in range(T // 2 // TB):
-                mine = pl.ds(pl.multiple_of(core * (T // 2) + k * TB, TB), TB)
-                tile = slice(k * TB, (k + 1) * TB)
+            for k in range(chunks):
+                self.near[k].wait_recv()
+                tile = slice(k * CH, (k + 1) * CH)
                 self.ch[xg, tile, :] = (
-                    ub[mine, :].astype(F32) + self.ra[tile, :].astype(F32)
+                    ub[half_rows(core, k), :].astype(F32) + self.ra[tile, :].astype(F32)
                 ).astype(BF16)
-            for one in self.far:
-                one.start()
+                for one in self.far[k]:
+                    one.start()
 
         def three(self):
-            for one in self.far:
-                one.wait_recv()
-            for k in range(T // 2 // TB):
-                tile = slice(k * TB, (k + 1) * TB)
+            for k in range(chunks):
+                for one in self.far[k]:
+                    one.wait_recv()
+                tile = slice(k * CH, (k + 1) * CH)
                 total = self.ch[0, tile, :].astype(F32)
                 for j in range(1, nx):
                     total += self.ch[j, tile, :].astype(F32)
                 self.fin[core, tile, :] = total.astype(BF16)
-            self.back.start()
+                self.back[k].start()
 
         def four(self):
-            self.back.wait_recv()
+            for one in self.back:
+                one.wait_recv()
 
         def drain(self):
-            for one in [*self.far, self.back]:
+            for far in self.far:
+                for one in far:
+                    one.wait_send()
+            for one in self.back:
                 one.wait_send()
 
     join_u = Join(ra, chU, finU)
     join_e = Join(ra, chE, finE)
-
-    for i in range(nb):
-        ctx_n = jnp.transpose(ctxT[i])
-        for k in range(B // TB):
-            rows = slice(i * B + k * TB, i * B + (k + 1) * TB)
-            ub[rows, :] = (
-                out[rows, :] + mm(ctx_n[k * TB : (k + 1) * TB], WT[3 * hs :, :])
-            ).astype(BF16)
-    join_u.one()
 
     dq[...] = jnp.zeros_like(dq)
 
@@ -522,10 +541,20 @@
         zero = jnp.zeros((HD, B), F32)
         put(lax.fori_loop(begin, end, query_step, (zero, zero)))
 
-    dkv_out = []
-    for r in range(1, nc):
-        owner = turn(c, nc - r, nc)
-        dkv_out.append(net.copy(kv.at[pl.ds(owner * nb, nb)], kv.at[own_blocks], (z, owner, t)))
+    dkv_base = net.used
+    net.used += (nc - 1) * nb
+
+    def dkv_copy(r, j):
+        owner, slot = turn(c, nc - r, nc), dkv_base + (r - 1) * nb + j
+        return pltpu.make_async_remote_copy(
+            src_ref=kv.at[owner * nb + j],
+            dst_ref=kv.at[c * nb + j],
+            send_sem=send.at[slot],
+            recv_sem=recv.at[slot],
+            device_id=(z, owner, t),
+            device_id_type=pl.DeviceIdType.MESH,
+        )
+
     for r in reversed(range(1, nc)):
 
         @pl.when(c >= r)
@@ -538,10 +567,20 @@
                         kv[(c - r) * nb + j, h, HD:] = pieces[1].astype(BF16)
 
                     key_back((c - r) * nb + j, h, put)
+                dkv_copy(r, j).start()
                 return carry
 
             lax.fori_loop(0, nb, block, 0)
-            dkv_out[r - 1].start()
+
+    for i in range(nb):
+        ctx_n = jnp.transpose(ctxT[i])
+        for k in range(B // TB):
+            rows = slice(i * B + k * TB, i * B + (k + 1) * TB)
+            ub[rows, :] = (
+                out[rows, :] + mm(ctx_n[k * TB : (k + 1) * TB], WT[hs : 2 * hs, :])
+            ).astype(BF16)
+    for one in join_u.near:
+        one.start()
 
     join_u.two()
 
@@ -556,6 +595,27 @@
         return carry
 
     lax.fori_loop(0, nb, own_block, 0)
+    def unrotated(g, i):
+        cb, sb = cosr[i], sinr[i]
+        lo, hi = g[:HALF], g[HALF:ROT]
+        return jnp.concatenate([lo * cb + hi * sb, hi * cb - lo * sb, g[ROT:]], 0)
+
+    bias_q = jnp.zeros((hs, 1), F32)
+    grad_o = None
+    for i in range(nb):
+        d_q = jnp.concatenate([unrotated(dq[i, h] * scale, i) for h in range(heads)], 0)
+        bias_q += jnp.sum(d_q, -1, keepdims=True)
+        d_q = d_q.astype(BF16)
+        tA[:hs, i * B : (i + 1) * B] = d_q
+        act[i * B : (i + 1) * B, : 2 * hs] = jnp.transpose(
+            jnp.concatenate([d_q, jnp.zeros_like(d_q)], 0)
+        )
+        term = mm(ctxT[i], gb[i * B : (i + 1) * B, :])
+        grad_o = term if grad_o is None else grad_o + term
+    grad_q = mm(tA[:hs, :], h1[...])
+    grad_a = jnp.transpose(jnp.concatenate([grad_q.astype(BF16), grad_o.astype(BF16)], 0))
+    store_grad(ggA, grad_a, 0)
+    redA.one()
     redB.two()
     join_u.three()
 
@@ -563,54 +623,43 @@
 
         @pl.when(c + r < nc)
         def _(r=r):
-            dkv_out[r - 1].wait_recv()
             for j in range(nb):
+                dkv_copy(r, j).wait_recv()
                 for h in range(heads):
                     dkv[j, h] += kv[(c + r) * nb + j, h].astype(F32)
 
-    grad_t = None
-    bias_t = jnp.zeros((3 * hs, 1), F32)
+    bias_kv = jnp.zeros((2 * hs, 1), F32)
     for i in range(nb):
-        cb, sb = cosr[i], sinr[i]
-
-        def unrotated(g):
-            lo, hi = g[:HALF], g[HALF:ROT]
-            return jnp.concatenate([lo * cb + hi * sb, hi * cb - lo * sb, g[ROT:]], 0)
-
-        pieces = [unrotated(dq[i, h] * scale) for h in range(heads)]
-        pieces += [unrotated(dkv[i, h, :HD]) for h in range(heads)]
+        pieces = [unrotated(dkv[i, h, :HD], i) for h in range(heads)]
         pieces += [dkv[i, h, HD:] for h in range(heads)]
-        d_proj = jnp.concatenate(pieces, 0)
-        bias_t += jnp.sum(d_proj, -1, keepdims=True)
-        d_proj_b = d_proj.astype(BF16)
-        tA[: 3 * hs, i * B : (i + 1) * B] = d_proj_b
-        act[i * B : (i + 1) * B, : 3 * hs] = jnp.transpose(d_proj_b)
+        d_kv = jnp.concatenate(pieces, 0)
+        bias_kv += jnp.sum(d_kv, -1, keepdims=True)
+        d_kv = d_kv.astype(BF16)
+        tA[2 * hs : 4 * hs, i * B : (i + 1) * B] = d_kv
+        act[i * B : (i + 1) * B, 2 * hs : 4 * hs] = jnp.transpose(d_kv)
+    bias_t = jnp.concatenate([bias_q, bias_kv], 0)
     sm[6:7, : 3 * hs] = jnp.transpose(jnp.broadcast_to(bias_t, (3 * hs, 128)))[0:1, :]
-
-    grad_q = mm(tA[: 3 * hs, :], h1[...])
-    grad_o = None
-    for i in range(nb):
-        term = mm(ctxT[i], gb[i * B : (i + 1) * B, :])
-        grad_o = term if grad_o is None else grad_o + term
-    grad_a = jnp.transpose(jnp.concatenate([grad_q.astype(BF16), grad_o.astype(BF16)], 0))
-    if not d.keep:
-        for one in [*redB.a, *redB.b]:
-            one.wait_send()
-    store_grad(ggA, grad_a, 0)
-    redA.one()
-    join_u.near.wait_send()
+    for one in join_u.near:
+        one.wait_send()
 
     def e_tile(i, carry):
         rows = tile_rows(i, TB)
-        dh1 = mm(act[rows, : 3 * hs], WT[: 3 * hs, :])
+        dh1 = mm(act[rows, :], WT[...])
         sm[0:1, :D] += jnp.sum(dh1 * normed_of(rows), 0, keepdims=True)
         sm[1:2, :D] += jnp.sum(dh1, 0, keepdims=True)
         ub[rows, :] = (ig[rows, :] + dh1 * g1).astype(BF16)
         return carry
 
-    lax.fori_loop(0, T // TB, e_tile, 0)
     join_u.four()
-    join_e.one()
+    for k in range(chunks):
+        for q in range(CH // TB):
+            for which in (1 - core, core):
+                e_tile(which * (T // 2 // TB) + k * (CH // TB) + q, 0)
+        join_e.near[k].start()
+    grad_kv = mm(tA[2 * hs : 4 * hs, :], h1[...])
+    store_grad(ggK, jnp.transpose(grad_kv.astype(BF16)), 0)
+    redK.one()
+    join_e.two()
     redC.three()
 
     rank = z * nc + c
@@ -624,9 +673,9 @@
                 )
     for one in small_a:
         one.start()
-    join_e.two()
+    redA.two()
     redB.three()
-    redA.two()
+    redK.two()
 
     put_u = pltpu.make_async_copy(finU, u_out, local.at[3])
     put_u.start()
@@ -643,6 +692,7 @@
     for one in small_b:
         one.start()
     redA.three()
+    redK.three()
     join_e.three()
     for one in small_b:
         one.wait_recv()
@@ -655,6 +705,7 @@
     put_e = pltpu.make_async_copy(finE, e_out, local.at[4])
     put_e.start()
     redA.four()
+    redK.four()
 
     for one in (gather_a, gather_b, gather_c):
         one.drain()
@@ -664,22 +715,24 @@
         def _(one=one):
             one.wait_send()
 
-    for r, one in enumerate(dkv_out, 1):
+    for r in range(1, nc):
 
         @pl.when(c >= r)
-        def _(one=one):
-            one.wait_send()
-
-    for one in redB.c if not d.keep else [*redB.a, *redB.b, *redB.c]:
-        one.wait_send()
+        def _(r=r):
+            for j in range(nb):
+                dkv_copy(r, j).wait_send()
+
+    redB.drain()
     redA.drain()
+    redK.drain()
     redC.drain()
     join_u.drain()
-    join_e.near.wait_send()
+    for one in join_e.near:
+        one.wait_send()
     join_e.drain()
     for one in [*small_a, *small_b]:
         one.wait_send()
-    for one in (redA.put, redB.put, redC.put, put_u, put_e):
+    for one in (redA.put, redB.put, redC.put, redK.put, put_u, put_e):
         one.wait()
     assert net.used == d.n_copies
 
@@ -736,36 +789,35 @@
         vm((d.nx, T // 2, D), BF16), vm((d.nx, T // 2, D), BF16),
         vm((2, T // 2, D), BF16), vm((2, T // 2, D), BF16),
     ]
-    widths = (wide_a, F, F)
-    piece = (HR, HR, R)
-    scratch += [vm((2, nz, HR, wide_a) if d.keep else (8, 128), BF16)]
-    scratch += [vm((2, nz, HR, F), BF16), vm((nz, R, F), BF16)]
-    scratch += [vm((nz, HR, w), BF16) for w in widths[:2]]
-    scratch += [vm((nz - 1, n, w), BF16) for n, w in zip(piece, widths)]
-    scratch += [vm((nc, n, w), BF16) for n, w in zip(piece, widths)]
+    owned_shapes = [(HR, 2 * hs), (HR, F), (R, F), (HR, 2 * hs)]
+    scratch += [vm((2, nz, HR, 2 * hs), BF16), vm((2, nz, HR, F), BF16)]
+    scratch += [vm((nz, R, F), BF16), vm((2, nz, HR, 2 * hs), BF16)]
+    scratch += [vm((nz, HR, w), BF16) for w in (2 * hs, F, 2 * hs)]
+    scratch += [vm((nz - 1, *shape), BF16) for shape in owned_shapes]
+    scratch += [vm((nc, *shape), BF16) for shape in owned_shapes]
     scratch += [vm((8, W), F32), vm((nz * nc, 8, W), F32), vm((d.nt, 8, W), F32)]
     scratch += [vm((T, D), F32), vm((T, D), F32), vm((R, wide_a), BF16)]
-    scratch += [vm((nb, HALF, B), F32), vm((nb, HALF, B), F32), vm((nb, 1, B), jnp.int32)]
-    scratch += [pltpu.SemaphoreType.DMA((n,)) for n in (d.n_copies, d.n_copies, 5)]
+    scratch += [vm((nb, HALF, B), F32), vm((nb, HALF, B), F32), vm((nb, 1, B), jnp.int32), vm((T, D), BF16)]
+    scratch += [pltpu.SemaphoreType.DMA((n,)) for n in (d.n_copies, d.n_copies, 8)]
 
     def kernel(*refs):
         layer_kernel(d, *refs)
 
     fin = jax.ShapeDtypeStruct((2, T // 2, D), BF16)
-    sums = [jax.ShapeDtypeStruct((nc, n, w), BF16) for n, w in zip(piece, widths)]
+    sums = [jax.ShapeDtypeStruct((nc, *shape), BF16) for shape in owned_shapes]
     in_hbm = pl.BlockSpec(memory_space=pl.ANY)
     joined, joined_e, *owned, small = pl.pallas_call(
         kernel,
         out_shape=(fin, fin, *sums, jax.ShapeDtypeStruct((8, W), F32)),
-        in_specs=[pl.BlockSpec(memory_space=vm)] * len(args),
-        out_specs=[in_hbm] * 5 + [pl.BlockSpec(memory_space=vm)],
+        in_specs=[in_hbm] * 2 + [pl.BlockSpec(memory_space=vm)] * (len(args) - 2),
+        out_specs=[in_hbm] * 6 + [pl.BlockSpec(memory_space=vm)],
         scratch_shapes=scratch,
         compiler_params=pltpu.CompilerParams(
             collective_id=0, has_side_effects=True, vmem_limit_bytes=VMEM_BYTES
         ),
     )(*args)
 
-    TB = d.tile
+    TB = d.blk
 
     def tiles():
         return pl.BlockSpec((TB, D), lambda i: (i, 0))
@@ -796,7 +848,7 @@
     return tuple(results)
 
 
-def finish_kernel(d, x, og, u, e, fa, fb, fc, small, bo, bf2, *outs):
+def finish_kernel(d, x, og, u, e, fa, fb, fc, fk, small, bo, bf2, *outs):
     out, ig, o_g1, o_b1, o_g2, o_b2, o_qkv, o_bqkv, o_wo, o_bo, o_fc1, o_bf1, o_fc2, o_bf2 = outs
     D, hs, F, HR = d.width, d.span, d.hidden, d.half
     xf = x[...].astype(F32)
@@ -819,16 +871,17 @@
     def _():
         for p in range(2):
             rows = slice(p * HR, (p + 1) * HR)
-            half_a = summed(fa, p)
-            for j in range(3):
-                o_qkv[j, rows, :] = half_a[:, j * hs : (j + 1) * hs]
+            o_qkv[0, rows, :] = summed(fa, p)[:, :hs]
+            half_k = summed(fk, p)
+            o_qkv[1, rows, :] = half_k[:, :hs]
+            o_qkv[2, rows, :] = half_k[:, hs:]
             o_fc1[rows, :] = summed(fb, p)
         total = fc[0].astype(F32)
         for j in range(1, d.nc):
             total += fc[j].astype(F32)
         o_fc2[...] = total
         whole_a = jnp.concatenate([summed(fa, 0), summed(fa, 1)], 0)
-        o_wo[...] = jnp.transpose(whole_a[:, 3 * hs :])
+        o_wo[...] = jnp.transpose(whole_a[:, hs:])
         for k, (o, n) in enumerate(
             ((o_g1, D), (o_b1, D), (o_g2, D), (o_b2, D), (o_bo, D), (o_bf1, F))
         ):

time: 138 us -> 137 us (level)
  no operation moved by 1% of the time
where the time goes in v3:
time: 137 us
  Pallas kernels  136 us (99%)
    pallas_call x1, Pallas kernels, body(): pl.pallas_call(kernel, out_shape=(fin, fin, *sums, jax.ShapeDtypeStruct((...  128 us
    pallas_call x1, Pallas kernels, body(): pl.pallas_call(lambda *refs: finish_kernel(d, *refs), grid=(T // TB,), ou...  7.71 us

profile of v3, /device:TPU:0, one launch (start us, length us, event | category | flops | bytes accessed | tf_op | source)
XLA Modules:
  0.0 136.9 jit_solution(8792901186210607937)
XLA Ops:
  0.6 128.4 %shard_map.254 = (bf16[2,512,768]{2,1,0:T(8,128)(2,1)}, bf16[2,512,768]{2,1,0:T(8,128)(2,1)}, bf16[2,96,384]{2,1,0:T(8,128)(2,1)}, bf16[2,96,768]{2,1,0:T(8,128)...) custom-call(bf16[1024,768]{1,0:T(8,128)(2,1)} %refs_0_.3, ...), custom_call_target="tpu_custom_call" | custom-call | tf_op jit(solution)/shard_map/pallas_call | solution.py:809
  129.0 7.7 %shard_map.255 = (f32[1024,768]{1,0:T(8,128)}, f32[1024,768]{1,0:T(8,128)}, f32[768]{0:T(1024)}, f32[768]{0:T(1024)}, f32[768]{0:T(1024)}, /*index=5*/f32[768]{0...) custom-call(bf16[1024,768]{1,0:T(8,128)(2,1)} %refs_0_.3, ...), custom_call_target="tpu_custom_call" | custom-call | tf_op jit(solution)/shard_map/pallas_call | solution.py:833
